TPU v7x, 512 devices: a whole 4x8x8 slice. The times are simulated.
512 devices in a mesh: dp: 64 (over y, x, core), mp: 8 (over z).
Axes of the slice: x: 4, y: 8, z: 8, core: 2. Of those that a mesh axis runs over, the one named last changes fastest.
Arguments:
- hidden: bfloat16 [960, 128, 2048], P('dp', None, 'mp'), may hold values from -6 to 6
- attn_out: bfloat16 [960, 128, 2048], P('dp', None, 'mp'), may hold values from -6 to 6
- out_proj: bfloat16 [2048, 2048], P(None, 'mp'), may hold values from -0.125 to 0.125
- norm_gain: float32 [2048], P('mp'), may hold values from 0.1 to 1.9
- reward_proj: float32 [2048, 8], P('mp'), may hold values from -0.125 to 0.125
- block_seq: int32 [960], replicated, may hold values from -1 to 383, as said below
- block_dest: int32 [960], replicated, may hold values from -1 to 639, as said below
- lengths: int32 [384], replicated, may hold values from 1 to 512, as said below
Outputs:
- token_rewards: float32 [640, 8, 128], P('dp')
- advantages: float32 [384], P('dp')
Inputs may be any that keep to these rules, and one draw needn't show every extreme that they name: `block_seq`: used slots of each index of dp come first in its 15 slots, the rest hold -1; each index of dp holds 1 to 15 used slots and some index holds exactly 15. Read over used slots in slot order, response numbers never fall, every response appears, and each has 1 to 4 blocks. `block_dest`: exactly the used slots (those of block_seq that are not -1) hold a destination; every owned slot of every owner is named exactly once, so each owner receives exactly 10 blocks; at most 1 block go from one index of dp to one owner, and that many in some pair. `lengths`: A response of n blocks has more than 128 * (n - 1) and at most 128 * n tokens.
All inputs are finite; a program needn't handle non-finite values.
Results may differ from a plain program's by a relative error of at most 0.0029.
Values may be sent and summed in bfloat16 or wider, within the bound.
No kernel may reach another device: no remote copies, remote signals or barrier semaphores. Data moves between devices by JAX's collectives and lax.ppermute only.
A program may use at most 64 MiB of HBM per device.

v0:
```python
import jax
import jax.numpy as jnp
from jax import lax
from jax.sharding import PartitionSpec as P

OWN_CAP = 10
norm_epsilon = 1e-05
stat_epsilon = 1e-06


def sent_to_all(value, axis):
    copies = jnp.broadcast_to(value, (lax.axis_size(axis), *value.shape))
    return lax.all_to_all(copies, axis, split_axis=0, concat_axis=0, tiled=True)


def of_everyone(value, axis):
    everything = sent_to_all(value, axis)
    return jnp.sum(everything, axis=0)


def packed_total(arrays, axis):
    ends = [0]
    for a in arrays:
        ends.append(ends[-1] + a.size)
    so_far = of_everyone(jnp.concatenate([a.ravel() for a in arrays]), axis)
    return tuple((so_far[b:e].reshape(a.shape) for a, b, e in zip(arrays, ends, ends[1:])))


def split_up(value, dim, peers):
    before, after = (value.shape[:dim], value.shape[dim + 1 :])
    return jnp.moveaxis(value.reshape(*before, peers, -1, *after), dim, 0)


def sent_and_summed(value, axis, dim):
    parts = split_up(value, dim, lax.axis_size(axis))
    arrived = lax.all_to_all(parts, axis, split_axis=0, concat_axis=0, tiled=True)
    return arrived.sum(axis=0)


def local(hidden, attn_out, out_proj, norm_gain, reward_proj, block_seq, block_dest, lengths):
    device_count = lax.axis_size("dp")
    device_rank = lax.axis_index("dp")
    slots_in = hidden.shape[0]
    block_len = hidden.shape[1]
    model_width = out_proj.shape[0]
    seq_count = lengths.shape[0]
    seq_local = seq_count // device_count
    slot_depth = (slots_in + device_count - 1) // device_count
    all_slots = jnp.arange(block_dest.shape[0], dtype=jnp.int32)
    local_dest = lax.dynamic_slice_in_dim(block_dest, device_rank * slots_in, slots_in)
    is_used = local_dest >= 0
    owner_rank = jnp.where(is_used, local_dest // OWN_CAP, -1)
    local_slots = jnp.arange(slots_in, dtype=jnp.int32)
    earlier = (
        (owner_rank[None, :] == owner_rank[:, None])
        & (local_slots[None, :] < local_slots[:, None])
        & is_used[None, :]
    )
    send_row = jnp.where(is_used, owner_rank * slot_depth + earlier.sum(axis=1), -1)
    buffer_rows = jnp.arange(device_count * slot_depth, dtype=jnp.int32)
    selector = (send_row[None, :] == buffer_rows[:, None]).astype(jnp.bfloat16)
    targets = device_rank * OWN_CAP + jnp.arange(OWN_CAP, dtype=jnp.int32)
    matches = block_dest[None, :] == targets[:, None]
    source_slot = jnp.sum(jnp.where(matches, all_slots[None, :], 0), axis=1)
    source_rank = source_slot // slots_in
    before = (block_dest[None, :] >= 0) & (block_dest[None, :] // OWN_CAP == device_rank)
    before = (
        before
        & (all_slots[None, :] >= (source_rank * slots_in)[:, None])
        & (all_slots[None, :] < source_slot[:, None])
    )
    recv_row = source_rank * slot_depth + before.sum(axis=1)
    seq_own = jnp.sum(jnp.where(matches, block_seq[None, :], 0), axis=1)
    earlier_same = (block_seq[None, :] == seq_own[:, None]) & (
        all_slots[None, :] < source_slot[:, None]
    )
    seq_rank = earlier_same.sum(axis=1)
    seq_ids = jnp.arange(seq_count, dtype=jnp.int32)
    member = seq_ids[:, None] == seq_own[None, :]
    own_length = jnp.sum(jnp.where(member, lengths[:, None], 0), axis=0)
    valid_tokens = jnp.minimum(block_len, own_length - block_len * seq_rank)
    projected = jnp.einsum(
        "btf,fc->btc",
        lax.all_gather(attn_out, "mp", axis=2, tiled=True),
        out_proj,
        preferred_element_type=jnp.float32,
    )
    local_resid = (hidden.astype(jnp.float32) + projected).astype(jnp.bfloat16)
    moved_resid = lax.all_to_all(
        jnp.einsum("rj,jtf->rtf", selector, local_resid, preferred_element_type=jnp.float32).astype(
            jnp.bfloat16
        ),
        "dp",
        split_axis=0,
        concat_axis=0,
        tiled=True,
    )
    residual = jnp.take(moved_resid, recv_row, axis=0)
    values = residual.astype(jnp.float32)
    squares = jnp.sum(values * values, axis=2)
    weighted = norm_gain[:, None] * reward_proj
    partial_value = jnp.einsum("btf,fh->bht", values, weighted, precision=lax.Precision.HIGHEST)
    squares, partial_value = packed_total((squares, partial_value), "mp")
    inverse_rms = lax.rsqrt(squares / model_width + norm_epsilon)
    live_tokens = (jnp.arange(block_len, dtype=jnp.int32)[None, :] < valid_tokens[:, None]).astype(
        jnp.float32
    )
    token_rewards = partial_value * (inverse_rms * live_tokens)[:, None, :]
    block_sums = jnp.sum(token_rewards, axis=2)
    seq_part = jnp.dot(member.astype(jnp.float32), block_sums, precision=lax.Precision.HIGHEST)
    seq_totals = sent_and_summed(seq_part, "dp", 0)
    own_lengths = lax.dynamic_slice_in_dim(lengths, device_rank * seq_local, seq_local).astype(
        jnp.float32
    )
    scores = seq_totals / own_lengths[:, None]
    worst_case = jnp.min(scores, axis=1)
    head_mean = jnp.mean(scores, axis=1)
    spread = jnp.mean((scores - head_mean[:, None]) ** 2, axis=1)
    total_seqs = float(seq_count)
    moment_sums = packed_total(
        (
            jnp.sum(spread),
            jnp.sum(worst_case),
            jnp.sum(worst_case * worst_case),
            jnp.sum(worst_case * spread),
            jnp.sum(spread * spread),
        ),
        "dp",
    )
    penalty_scale = moment_sums[0] / total_seqs + stat_epsilon
    conservative = worst_case - spread / penalty_scale
    first_sum = moment_sums[1] - moment_sums[0] / penalty_scale
    second = (
        moment_sums[2]
        - 2.0 * moment_sums[3] / penalty_scale
        + moment_sums[4] / (penalty_scale * penalty_scale)
    )
    centre = first_sum / total_seqs
    variance = second / total_seqs - centre * centre
    advantages = (conservative - centre) * lax.rsqrt(variance + stat_epsilon)
    return (token_rewards, advantages)


def solution(mesh):
    return jax.shard_map(
        local,
        mesh=mesh,
        in_specs=(
            P("dp", None, "mp"),
            P("dp", None, "mp"),
            P(None, "mp"),
            P("mp"),
            P("mp", None),
            P(),
            P(),
            P(),
        ),
        out_specs=(P("dp", None, None), P("dp")),
        check_vma=False,
    )
```

profile of v0, /device:TPU:1, one launch (start us, length us, event | category | flops | bytes accessed | tf_op | source)
XLA Modules:
  0.0 305.1 jit_solution(17338030331236136521)
XLA Ops:
  7.2 0.0 copy-start
  7.2 0.0 all-gather.2.cloned.1.call-start
  7.2 0.7 all-gather.2.cloned.1.call-update
  7.9 0.8 fusion.29
  8.7 0.2 convert_reduce_fusion.2
  8.9 101.2 %all-gather.2.cloned.1.call-done = bf16[15,128,2048]{2,1,0:T(8,128)(2,1)} async-done(((bf16[15,128,256]{2,1,0:T(8,128)(2,1)}), bf16[15,128,2048]{2,1,0:T(8,128)(2,1)}) %all-gather.2.cloned.1.call-update) | async-done | bytes 7864336 | tf_op jit(solution)/shard_map/all_gather | solution.py:84
  110.1 0.0 copy-done
  110.1 5.7 %add_convert_fusion = bf16[15,128,256]{2,1,0:T(8,128)(2,1)S(1)} fusion(bf16[15,128,256]{2,1,0:T(8,128)(2,1)} %param.8, bf16[15,128,2048]{2,1,0:T(8,128)(2,1)} %all-gather.2.cloned.1.call-done, bf16[2048,256]{1,0:T(8,128)(2,1)S(1)} %copy-done), kind=kOutput, calls=%fused_computation.3 | convolution fusion | flops 2014740480 | bytes 10878976 | tf_op jit(solution)/shard_map/btf,fc->btc/dot_general | solution.py:82
  115.8 1.4 convolution_convert_fusion
  117.1 4.4 %copy.29 = bf16[64,128,256]{2,1,0:T(8,128)(2,1)} copy(bf16[64,128,256]{2,0,1:T(8,128)(2,1)S(1)} %convolution_convert_fusion) | data formatting | bytes 8388608 | tf_op jit(solution)/shard_map/convert_element_type | solution.py:90
  121.5 0.0 copy-start.1
  121.5 0.0 copy-start.2
  121.5 0.0 copy-start.4
  121.5 0.0 copy-start.5
  121.5 13.3 %all-to-all-start = ((bf16[64,128,256]{2,1,0:T(8,128)(2,1)}), bf16[64,128,256]{2,1,0:T(8,128)(2,1)}, u32[]{:S(2)}, u32[]{:S(2)}) async-start(bf16[64,128,256]{2,1,0:T(8,128)(2,1)} %copy.29), calls=%async_computation | async-start | bytes 8388608 | tf_op jit(solution)/shard_map/all_to_all | solution.py:89
  134.8 0.0 copy-start.3
  134.9 0.0 copy-done.1
  134.9 0.0 copy-done.2
  134.9 0.2 fusion.3
  135.1 0.2 convert_reduce_fusion
  135.4 94.2 %all-to-all-done = bf16[64,128,256]{2,1,0:T(8,128)(2,1)} async-done(((bf16[64,128,256]{2,1,0:T(8,128)(2,1)}), bf16[64,128,256]{2,1,0:T(8,128)(2,1)}, u32[]{:S(2)}, u32[]{:S(2)}) %all-to-all-start) | async-done | bytes 4194336 | tf_op jit(solution)/shard_map/all_to_all | solution.py:89
  229.5 2.8 gather_fusion
  232.3 0.3 multiply_reduce_fusion
  232.7 0.0 copy-done.4
  232.7 0.0 copy-done.5
  232.7 0.7 convolution_bitcast_fusion
  233.4 0.9 broadcast_in_dim.89
  234.3 3.9 %all-to-all-start.1 = ((f32[8,1,11520]{2,1,0:T(1,128)}), f32[8,1,11520]{2,1,0:T(1,128)S(1)}, u32[]{:S(2)}, u32[]{:S(2)}) async-start(f32[8,1,11520]{2,1,0:T(1,128)} %broadcast_in_dim.89), calls=%async_computation.1 | async-start | bytes 737280 | tf_op jit(solution)/shard_map/all_to_all | solution.py:13
  238.2 0.0 copy-done.3
  238.2 0.2 select_reduce_fusion
  238.4 11.5 %all-to-all-done.1 = f32[8,1,11520]{2,1,0:T(1,128)S(1)} async-done(((f32[8,1,11520]{2,1,0:T(1,128)}), f32[8,1,11520]{2,1,0:T(1,128)S(1)}, u32[]{:S(2)}, u32[]{:S(2)}) %all-to-all-start.1) | async-done | bytes 368672 | tf_op jit(solution)/shard_map/all_to_all | solution.py:13
  249.9 0.3 reduce_sum.169
  250.2 0.1 fusion.15
  250.2 0.6 fusion.34
  250.9 0.2 fusion.7
  251.1 0.8 copy.32
  251.9 9.6 %all-to-all-start.2 = ((f32[64,6,8]{2,1,0:T(8,128)}), f32[64,6,8]{2,1,0:T(8,128)S(1)}, u32[]{:S(2)}, u32[]{:S(2)}) async-start(f32[64,6,8]{2,1,0:T(8,128)} %copy.32), calls=%async_computation.2 | async-start | bytes 524288 | tf_op jit(solution)/shard_map/all_to_all | solution.py:36
  261.6 0.1 dynamic-slice_convert_fusion
  261.6 13.0 %all-to-all-done.2 = f32[64,6,8]{2,1,0:T(8,128)S(1)} async-done(((f32[64,6,8]{2,1,0:T(8,128)}), f32[64,6,8]{2,1,0:T(8,128)S(1)}, u32[]{:S(2)}, u32[]{:S(2)}) %all-to-all-start.2) | async-done | bytes 12320 | tf_op jit(solution)/shard_map/all_to_all | solution.py:36
  274.6 0.1 reduce_sum.174
  274.7 0.2 fusion.32
  274.9 0.2 multiply_reduce_fusion.1
  275.1 0.7 multiply_reduce_fusion.2
  275.8 3.2 %concatenate.7 = f32[5]{0:T(128)S(1)} concatenate(f32[1]{0:T(128)} %bitcast.13, f32[1]{0:T(128)} %bitcast.14, f32[1]{0:T(128)} %bitcast.15, f32[1]{0:T(128)} %bitcast.16, f32[1]{0:T(128)} %bitcast.17), dimensions={0} | concatenate | bytes 40 | tf_op jit(solution)/shard_map/concatenate | solution.py:25
  279.1 14.0 %all_to_all.22 = f32[64,1,5]{2,1,0:T(1,128)S(1)} all-to-all(f32[64,1,5]{2,1,0:T(1,128)S(1)} %broadcast_in_dim.93), channel_id=1, replica_groups=mesh['dp'=64,'mp'=8] {'dp'}, dimensions={0} | all-to-all | bytes 2560 | tf_op jit(solution)/shard_map/all_to_all | solution.py:13
  293.1 0.1 reduce_sum.182
  293.1 0.7 fusion.36
  297.7 0.5 subtract_multiply_fusion
  (12 shorter events, 0.1 us)
Async XLA Ops:
  7.2 102.9 %copy-start = (bf16[2048,256]{1,0:T(8,128)(2,1)S(1)}, bf16[2048,256]{1,0:T(8,128)(2,1)}, u32[]{:S(2)}) copy-start(bf16[2048,256]{1,0:T(8,128)(2,1)} %param.10) | copy-start | bytes 3145732
  7.2 102.9 %all-gather.2.cloned.1.call-start = ((), (), s32[]{:S(2)}) async-start(), calls=%async_computation.4 | async-start | bytes 8847360 | tf_op jit(solution)/shard_map/all_gather | solution.py:84
  121.5 13.3 %copy-start.1 = (s32[960]{0:T(1024)S(1)}, s32[960]{0:T(1024)}, u32[]{:S(2)}) copy-start(s32[960]{0:T(1024)} %param.14) | copy-start | bytes 11524
  121.5 13.3 %copy-start.2 = (s32[960]{0:T(1024)S(1)}, s32[960]{0:T(1024)}, u32[]{:S(2)}) copy-start(s32[960]{0:T(1024)} %param.13) | copy-start | bytes 11524
  121.5 111.1 %copy-start.4 = (f32[256,8]{0,1:T(8,128)S(1)}, f32[256,8]{0,1:T(8,128)}, u32[]{:S(2)}) copy-start(f32[256,8]{0,1:T(8,128)} %param.12) | copy-start | bytes 24580
  121.5 111.1 %copy-start.5 = (f32[256]{0:T(256)S(1)}, f32[256]{0:T(256)}, u32[]{:S(2)}) copy-start(f32[256]{0:T(256)} %param.11) | copy-start | bytes 3076
  121.5 108.0 %all-to-all-start = ((bf16[64,128,256]{2,1,0:T(8,128)(2,1)}), bf16[64,128,256]{2,1,0:T(8,128)(2,1)}, u32[]{:S(2)}, u32[]{:S(2)}) async-start(bf16[64,128,256]{2,1,0:T(8,128)(2,1)} %copy.29), calls=%async_computation | async-start | bytes 8388608 | tf_op jit(solution)/shard_map/all_to_all | solution.py:89
  134.8 103.4 %copy-start.3 = (s32[384]{0:T(512)S(1)}, s32[384]{0:T(512)}, u32[]{:S(2)}) copy-start(s32[384]{0:T(512)} %param.15) | copy-start | bytes 4612
  234.3 15.6 %all-to-all-start.1 = ((f32[8,1,11520]{2,1,0:T(1,128)}), f32[8,1,11520]{2,1,0:T(1,128)S(1)}, u32[]{:S(2)}, u32[]{:S(2)}) async-start(f32[8,1,11520]{2,1,0:T(1,128)} %broadcast_in_dim.89), calls=%async_computation.1 | async-start | bytes 737280 | tf_op jit(solution)/shard_map/all_to_all | solution.py:13
  251.9 22.7 %all-to-all-start.2 = ((f32[64,6,8]{2,1,0:T(8,128)}), f32[64,6,8]{2,1,0:T(8,128)S(1)}, u32[]{:S(2)}, u32[]{:S(2)}) async-start(f32[64,6,8]{2,1,0:T(8,128)} %copy.32), calls=%async_computation.2 | async-start | bytes 524288 | tf_op jit(solution)/shard_map/all_to_all | solution.py:36
Sparse Core Ops, SparseCore 0:
  10.0 100.0 all-gather.1
where the time goes:
time: 306 us; the launch traced here: 305 us
  waiting for transfers between devices  221 us (72%)
  starting transfers between devices  26.8 us (9%)
  between operations  18.1 us (6%)
  blocking collectives  14 us (5%)
  local copies, waits for them, and re-layouts  12.9 us (4%)
  matrix products  7.93 us (3%)
  other arithmetic  4.83 us (2%)
    all_gather x1, waiting for transfers between devices, local(): lax.all_gather(attn_out, 'mp', axis=2, tiled=True)  101 us
    all_to_all x1, waiting for transfers between devices, local(): lax.all_to_all(jnp.einsum('rj,jtf->rtf', selector, local_resid, preferred...  94.2 us
    all_to_all x1, blocking collectives, sent_to_all(): return lax.all_to_all(copies, axis, split_axis=0, concat_axis=0, tiled=True)  14 us
    all_to_all x1, starting transfers between devices, local(): lax.all_to_all(jnp.einsum('rj,jtf->rtf', selector, local_resid, preferred...  13.3 us
    all_to_all x1, waiting for transfers between devices, sent_and_summed(): lax.all_to_all(parts, axis, split_axis=0, concat_axis=0, tiled=True)  13 us
    all_to_all x1, waiting for transfers between devices, sent_to_all(): return lax.all_to_all(copies, axis, split_axis=0, concat_axis=0, tiled=True)  11.5 us
    all_to_all x1, starting transfers between devices, sent_and_summed(): lax.all_to_all(parts, axis, split_axis=0, concat_axis=0, tiled=True)  9.64 us
  transfers between devices with their start and end apart: 4, of which 4 were waited for; matrix products, arithmetic and copies ran while one was open for 1% of the time, Pallas kernels for 0%

commit v1 on v0

--- a/solution.py
+++ b/solution.py
@@ -1,11 +1,42 @@
+import functools
 import jax
 import jax.numpy as jnp
 from jax import lax
 from jax.sharding import PartitionSpec as P
+from jax.lax import axis_index, axis_size, ppermute
 
 OWN_CAP = 10
 norm_epsilon = 1e-05
 stat_epsilon = 1e-06
+
+
+def render_pools(u_in, d0):
+    heard = list(u_in.shape[1:])
+    heard[d0] *= u_in.shape[0]
+    return jnp.moveaxis(u_in, 0, d0).reshape(heard)
+
+
+def follow_the_pairs_all(shard_in, device_axis, axis_k):
+    n_slots = axis_size(device_axis)
+    buffers = [(d, (d + 1) % n_slots) for d in range(n_slots)]
+    panels = [(dev_j, k0) for k0, dev_j in buffers]
+    f_next, r_now = ([], [])
+    for it in range(n_slots - 1):
+        if it % 2 == 0:
+            t1 = ppermute(f_next[-1] if f_next else shard_in, device_axis, buffers)
+            f_next.append(t1)
+        else:
+            res = ppermute(r_now[-1] if r_now else shard_in, device_axis, panels)
+            r_now.append(res)
+    mat_out = jnp.stack([*f_next[::-1], shard_in, *r_now])
+    t_next = axis_index(device_axis)
+    plain = len(f_next)
+    next_value = t_next - plain
+    mat_out = mat_out[(jnp.arange(n_slots) - next_value) % n_slots]
+    return render_pools(mat_out, axis_k)
+
+
+load_patches = functools.partial(follow_the_pairs_all, device_axis="mp", axis_k=2)
 
 
 def sent_to_all(value, axis):
@@ -80,10 +111,7 @@
     own_length = jnp.sum(jnp.where(member, lengths[:, None], 0), axis=0)
     valid_tokens = jnp.minimum(block_len, own_length - block_len * seq_rank)
     projected = jnp.einsum(
-        "btf,fc->btc",
-        lax.all_gather(attn_out, "mp", axis=2, tiled=True),
-        out_proj,
-        preferred_element_type=jnp.float32,
+        "btf,fc->btc", load_patches(attn_out), out_proj, preferred_element_type=jnp.float32
     )
     local_resid = (hidden.astype(jnp.float32) + projected).astype(jnp.bfloat16)
     moved_resid = lax.all_to_all(

time: 306 us -> 331 us (1.082)
  local copies, waits for them, and re-layouts: 12.9 us -> 46.7 us
  starting transfers between devices: 26.8 us -> 51.6 us
  waiting for transfers between devices: 221 us -> 200 us
  between operations: 18.1 us -> 4.82 us
    all_gather x1 -> x0, waiting for transfers between devices: 101 us -> none  [local(): lax.all_gather(attn_out, 'mp', axis=2, tiled=True)]
    ppermute x0 -> x7, waiting for transfers between devices: none -> 81.1 us  [the longest x4 81.1 us: follow_the_pairs_all(): t1 = ppermute(f_next[-1] if f_next else shard_in, device_axis, buffers)]
    ppermute x0 -> x7, starting transfers between devices: none -> 24.4 us  [the longest x3 13.7 us: follow_the_pairs_all(): res = ppermute(r_now[-1] if r_now else shard_in, device_axis, panels)]
    unnamed x12 -> x25, local copies, waits for them, and re-layouts: 0.03 us -> 14.4 us
    transpose x0 -> x1, local copies, waits for them, and re-layouts: none -> 10.7 us  [render_pools(): return jnp.moveaxis(u_in, 0, d0).reshape(heard)]
    gather x0 -> x1, local copies, waits for them, and re-layouts: none -> 7.8 us  [follow_the_pairs_all(): mat_out = mat_out[(jnp.arange(n_slots) - next_value) % n_slots]]
  transfers between devices with their start and end apart: 4 -> 10, of which waited for: 4 -> 7; matrix products, arithmetic and copies ran while one was open for 1% -> 5% of each run, Pallas kernels for 0% -> 0%
where the time goes in v1:
time: 331 us; the launch traced here: 330 us
  waiting for transfers between devices  200 us (60%)
  starting transfers between devices  51.6 us (16%)
  local copies, waits for them, and re-layouts  46.7 us (14%)
  blocking collectives  14 us (4%)
  matrix products  7.76 us (2%)
  other arithmetic  4.85 us (1%)
  between operations  4.82 us (1%)
    all_to_all x1, waiting for transfers between devices, local(): lax.all_to_all(jnp.einsum('rj,jtf->rtf', selector, local_resid, preferred...  94.2 us
    ppermute x4, waiting for transfers between devices, follow_the_pairs_all(): t1 = ppermute(f_next[-1] if f_next else shard_in, device_axis, buffers)  81.1 us
    unnamed x25, local copies, waits for them, and re-layouts  14.4 us
    all_to_all x1, starting transfers between devices, local(): lax.all_to_all(jnp.einsum('rj,jtf->rtf', selector, local_resid, preferred...  14.3 us
    all_to_all x1, blocking collectives, sent_to_all(): return lax.all_to_all(copies, axis, split_axis=0, concat_axis=0, tiled=True)  14 us
    ppermute x3, starting transfers between devices, follow_the_pairs_all(): res = ppermute(r_now[-1] if r_now else shard_in, device_axis, panels)  13.7 us
    all_to_all x1, waiting for transfers between devices, sent_and_summed(): lax.all_to_all(parts, axis, split_axis=0, concat_axis=0, tiled=True)  13 us
    all_to_all x1, waiting for transfers between devices, sent_to_all(): return lax.all_to_all(copies, axis, split_axis=0, concat_axis=0, tiled=True)  11.6 us
  transfers between devices with their start and end apart: 10, of which 7 were waited for; matrix products, arithmetic and copies ran while one was open for 5% of the time, Pallas kernels for 0%

profile of v1, /device:TPU:1, one launch (start us, length us, event | category | flops | bytes accessed | tf_op | source)
XLA Modules:
  0.0 329.6 jit_solution(14798518004675377240)
XLA Ops:
  0.6 0.0 copy-start
  0.7 4.9 %collective-permute-start = (bf16[15,128,256]{2,1,0:T(8,128)(2,1)}, bf16[15,128,256]{2,1,0:T(8,128)(2,1)S(1)}, u32[]{:S(2)}, u32[]{:S(2)}) collective-permute-start(bf16[15,128,256]{2,1,0:T(8,128)(2,1)} %param.9), channel_id=1, source_target_pairs={{0,1},{1,2},{2,3},{3,4},{4,5},{5,6},{6,7},{7,0},{8,9},{9,10},{10,1... | collective-permute-start | bytes 2949128 | tf_op jit(solution)/shard_map/ppermute | solution.py:26
  5.6 28.3 %collective-permute-done = bf16[15,128,256]{2,1,0:T(8,128)(2,1)S(1)} collective-permute-done((bf16[15,128,256]{2,1,0:T(8,128)(2,1)}, bf16[15,128,256]{2,1,0:T(8,128)(2,1)S(1)}, u32[]{:S(2)}, u32[]{:S(2)}) %collective-permute-start) | collective-permute-done | bytes 983072 | tf_op jit(solution)/shard_map/ppermute | solution.py:26
  33.9 1.9 collective-permute-start.1
  35.9 4.6 %collective-permute-start.4 = (bf16[15,128,256]{2,1,0:T(8,128)(2,1)}, bf16[15,128,256]{2,1,0:T(8,128)(2,1)}, u32[]{:S(2)}, u32[]{:S(2)}) collective-permute-start(bf16[15,128,256]{2,1,0:T(8,128)(2,1)} %param.9), channel_id=1, source_target_pairs={{1,0},{2,1},{3,2},{4,3},{5,4},{6,5},{7,6},{0,7},{9,8},{10,9},{11,1... | collective-permute-start | bytes 2949128 | tf_op jit(solution)/shard_map/ppermute | solution.py:29
  40.4 18.7 %collective-permute-done.1 = bf16[15,128,256]{2,1,0:T(8,128)(2,1)S(1)} collective-permute-done((bf16[15,128,256]{2,1,0:T(8,128)(2,1)S(1)}, bf16[15,128,256]{2,1,0:T(8,128)(2,1)S(1)}, u32[]{:S(2)}, u32[]{:S(2)}) %collective-permute-start.1) | collective-permute-done | bytes 983072 | tf_op jit(solution)/shard_map/ppermute | solution.py:26
  59.1 1.0 copy-done.3
  60.1 1.9 collective-permute-start.2
  62.0 0.0 collective-permute-done.4
  62.0 4.6 %collective-permute-start.5 = (bf16[15,128,256]{2,1,0:T(8,128)(2,1)}, bf16[15,128,256]{2,1,0:T(8,128)(2,1)}, u32[]{:S(2)}, u32[]{:S(2)}) collective-permute-start(bf16[15,128,256]{2,1,0:T(8,128)(2,1)} %collective-permute-done.4), channel_id=1, source_target_pairs={{1,0},{2,1},{3,2},{4,3},{5,4},{6,5},{7,6},{0,7},{9,8},{10,9},{11,1... | collective-permute-start | bytes 2949128 | tf_op jit(solution)/shard_map/ppermute | solution.py:29
  66.6 17.9 %collective-permute-done.2 = bf16[15,128,256]{2,1,0:T(8,128)(2,1)} collective-permute-done((bf16[15,128,256]{2,1,0:T(8,128)(2,1)S(1)}, bf16[15,128,256]{2,1,0:T(8,128)(2,1)}, u32[]{:S(2)}, u32[]{:S(2)}) %collective-permute-start.2) | collective-permute-done | bytes 983072 | tf_op jit(solution)/shard_map/ppermute | solution.py:26
  84.5 1.9 collective-permute-start.3
  86.4 0.8 fusion.31
  87.2 0.2 convert_reduce_fusion.2
  87.4 0.0 collective-permute-done.5
  87.4 4.6 %collective-permute-start.6 = (bf16[15,128,256]{2,1,0:T(8,128)(2,1)}, bf16[15,128,256]{2,1,0:T(8,128)(2,1)S(1)}, u32[]{:S(2)}, u32[]{:S(2)}) collective-permute-start(bf16[15,128,256]{2,1,0:T(8,128)(2,1)} %collective-permute-done.5), channel_id=1, source_target_pairs={{1,0},{2,1},{3,2},{4,3},{5,4},{6,5},{7,6},{0,7},{9,8},{10,9},{11,1... | collective-permute-start | bytes 2949128 | tf_op jit(solution)/shard_map/ppermute | solution.py:29
  92.0 16.3 %collective-permute-done.3 = bf16[15,128,256]{2,1,0:T(8,128)(2,1)} collective-permute-done((bf16[15,128,256]{2,1,0:T(8,128)(2,1)}, bf16[15,128,256]{2,1,0:T(8,128)(2,1)}, u32[]{:S(2)}, u32[]{:S(2)}) %collective-permute-start.3) | collective-permute-done | bytes 983072 | tf_op jit(solution)/shard_map/ppermute | solution.py:26
  108.2 2.2 bitcast_dynamic-update-slice_fusion.7
  110.5 2.3 bitcast_dynamic-update-slice_fusion.6
  112.7 2.3 bitcast_dynamic-update-slice_fusion.5
  115.0 1.0 bitcast_dynamic-update-slice_fusion.4
  116.0 1.0 bitcast_dynamic-update-slice_fusion.3
  117.0 2.3 bitcast_dynamic-update-slice_fusion.2
  119.3 2.3 bitcast_dynamic-update-slice_fusion.1
  121.6 0.0 collective-permute-done.6
  121.6 1.0 bitcast_dynamic-update-slice_fusion
  122.6 7.8 %gather_fusion = bf16[8,15,128,256]{3,2,1,0:T(8,128)(2,1)} fusion(bf16[8,15,128,256]{3,2,1,0:T(8,128)(2,1)} %bitcast_dynamic-update-slice_fusion, s32[1024]{0:T(1024)S(1)} %pad_clamp_fusion.1), kind=kCustom, calls=%fused_computation | custom fusion | bytes 15728672 | tf_op jit(solution)/shard_map/gather | solution.py:35
  130.4 10.7 %copy.38 = bf16[15,128,8,256]{1,3,2,0:T(8,128)(2,1)} copy(bf16[15,128,8,256]{3,1,0,2:T(8,128)(2,1)} %bitcast.74) | data formatting | bytes 15728640 | tf_op jit(solution)/shard_map/transpose | solution.py:16
  141.1 0.0 copy-done
  141.1 5.5 %add_convert_fusion = bf16[15,128,256]{2,1,0:T(8,128)(2,1)S(1)} fusion(bf16[15,128,256]{2,1,0:T(8,128)(2,1)S(1)} %copy-done.1, bf16[15,128,2048]{1,2,0:T(8,128)(2,1)} %bitcast.73, bf16[2048,256]{1,0:T(8,128)(2,1)S(1)} %copy-done), kind=kOutput, calls=%fused_computation.4 | convolution fusion | flops 2014740480 | bytes 10878976 | tf_op jit(solution)/shard_map/btf,fc->btc/dot_general | solution.py:113
  146.6 1.4 convolution_convert_fusion
  148.0 0.0 copy-start.4
  148.0 0.0 copy-start.5
  148.0 0.0 copy-start.7
  148.0 0.0 copy-start.8
  148.0 4.4 %copy.41 = bf16[64,128,256]{2,1,0:T(8,128)(2,1)} copy(bf16[64,128,256]{2,0,1:T(8,128)(2,1)S(1)} %convolution_convert_fusion) | data formatting | bytes 8388608 | tf_op jit(solution)/shard_map/convert_element_type | solution.py:118
  152.4 14.3 %all-to-all-start = ((bf16[64,128,256]{2,1,0:T(8,128)(2,1)}), bf16[64,128,256]{2,1,0:T(8,128)(2,1)}, u32[]{:S(2)}, u32[]{:S(2)}) async-start(bf16[64,128,256]{2,1,0:T(8,128)(2,1)} %copy.41), calls=%async_computation | async-start | bytes 8388608 | tf_op jit(solution)/shard_map/all_to_all | solution.py:117
  166.7 0.2 fusion.3
  167.0 0.2 convert_reduce_fusion
  167.2 94.2 %all-to-all-done = bf16[64,128,256]{2,1,0:T(8,128)(2,1)} async-done(((bf16[64,128,256]{2,1,0:T(8,128)(2,1)}), bf16[64,128,256]{2,1,0:T(8,128)(2,1)}, u32[]{:S(2)}, u32[]{:S(2)}) %all-to-all-start) | async-done | bytes 4194336 | tf_op jit(solution)/shard_map/all_to_all | solution.py:117
  261.4 2.8 gather_fusion.1
  264.2 0.3 multiply_reduce_fusion
  264.5 0.7 convolution_bitcast_fusion
  265.3 0.9 broadcast_in_dim.90
  266.2 3.4 %all-to-all-start.1 = ((f32[8,1,11520]{2,1,0:T(1,128)}), f32[8,1,11520]{2,1,0:T(1,128)S(1)}, u32[]{:S(2)}, u32[]{:S(2)}) async-start(f32[8,1,11520]{2,1,0:T(1,128)} %broadcast_in_dim.90), calls=%async_computation.1 | async-start | bytes 737280 | tf_op jit(solution)/shard_map/all_to_all | solution.py:44
  269.7 0.2 select_reduce_fusion
  269.9 11.6 %all-to-all-done.1 = f32[8,1,11520]{2,1,0:T(1,128)S(1)} async-done(((f32[8,1,11520]{2,1,0:T(1,128)}), f32[8,1,11520]{2,1,0:T(1,128)S(1)}, u32[]{:S(2)}, u32[]{:S(2)}) %all-to-all-start.1) | async-done | bytes 368672 | tf_op jit(solution)/shard_map/all_to_all | solution.py:44
  281.4 0.3 reduce_sum.169
  281.7 0.1 fusion.15
  281.8 0.6 fusion.36
  282.4 0.2 fusion.7
  282.6 0.8 copy.44
  283.4 9.5 %all-to-all-start.2 = ((f32[64,6,8]{2,1,0:T(8,128)}), f32[64,6,8]{2,1,0:T(8,128)S(1)}, u32[]{:S(2)}, u32[]{:S(2)}) async-start(f32[64,6,8]{2,1,0:T(8,128)} %copy.44), calls=%async_computation.2 | async-start | bytes 524288 | tf_op jit(solution)/shard_map/all_to_all | solution.py:67
  292.9 0.1 dynamic-slice_convert_fusion
  293.0 13.0 %all-to-all-done.2 = f32[64,6,8]{2,1,0:T(8,128)S(1)} async-done(((f32[64,6,8]{2,1,0:T(8,128)}), f32[64,6,8]{2,1,0:T(8,128)S(1)}, u32[]{:S(2)}, u32[]{:S(2)}) %all-to-all-start.2) | async-done | bytes 12320 | tf_op jit(solution)/shard_map/all_to_all | solution.py:67
  306.0 0.1 reduce_sum.174
  306.1 0.2 fusion.34
  306.2 0.2 multiply_reduce_fusion.1
  306.5 0.7 multiply_reduce_fusion.2
  307.2 3.2 concatenate.7
  310.4 14.0 %all_to_all.22 = f32[64,1,5]{2,1,0:T(1,128)S(1)} all-to-all(f32[64,1,5]{2,1,0:T(1,128)S(1)} %broadcast_in_dim.94), channel_id=1, replica_groups=mesh['dp'=64,'mp'=8] {'dp'}, dimensions={0} | all-to-all | bytes 2560 | tf_op jit(solution)/shard_map/all_to_all | solution.py:44
  324.4 0.1 reduce_sum.182
  324.5 0.7 fusion.38
  329.1 0.5 subtract_multiply_fusion
  (25 shorter events, 0.2 us)
Async XLA Ops:
  0.6 140.5 %copy-start = (bf16[2048,256]{1,0:T(8,128)(2,1)S(1)}, bf16[2048,256]{1,0:T(8,128)(2,1)}, u32[]{:S(2)}) copy-start(bf16[2048,256]{1,0:T(8,128)(2,1)} %param.10) | copy-start | bytes 3145732
  0.6 115.4 %copy-start.2 = (bf16[15,128,256]{2,1,0:T(8,128)(2,1)S(1)}, bf16[15,128,256]{2,1,0:T(8,128)(2,1)}, u32[]{:S(2)}) copy-start(bf16[15,128,256]{2,1,0:T(8,128)(2,1)} %param.9) | copy-start | bytes 2949124
  0.7 33.3 %collective-permute-start = (bf16[15,128,256]{2,1,0:T(8,128)(2,1)}, bf16[15,128,256]{2,1,0:T(8,128)(2,1)S(1)}, u32[]{:S(2)}, u32[]{:S(2)}) collective-permute-start(bf16[15,128,256]{2,1,0:T(8,128)(2,1)} %param.9), channel_id=1, source_target_pairs={{0,1},{1,2},{2,3},{3,4},{4,5},{5,6},{6,7},{7,0},{8,9},{9,10},{10,1... | collective-permute-start | bytes 2949128 | tf_op jit(solution)/shard_map/ppermute | solution.py:26
  33.9 25.2 %collective-permute-start.1 = (bf16[15,128,256]{2,1,0:T(8,128)(2,1)S(1)}, bf16[15,128,256]{2,1,0:T(8,128)(2,1)S(1)}, u32[]{:S(2)}, u32[]{:S(2)}) collective-permute-start(bf16[15,128,256]{2,1,0:T(8,128)(2,1)S(1)} %collective-permute-done), channel_id=1, source_target_pairs={{0,1},{1,2},{2,3},{3,4},{4,5},{5,6},{6,7},{7,0},{8,9},{9,10},{10,1... | collective-permute-start | bytes 2949128 | tf_op jit(solution)/shard_map/ppermute | solution.py:26
  35.9 26.1 %collective-permute-start.4 = (bf16[15,128,256]{2,1,0:T(8,128)(2,1)}, bf16[15,128,256]{2,1,0:T(8,128)(2,1)}, u32[]{:S(2)}, u32[]{:S(2)}) collective-permute-start(bf16[15,128,256]{2,1,0:T(8,128)(2,1)} %param.9), channel_id=1, source_target_pairs={{1,0},{2,1},{3,2},{4,3},{5,4},{6,5},{7,6},{0,7},{9,8},{10,9},{11,1... | collective-permute-start | bytes 2949128 | tf_op jit(solution)/shard_map/ppermute | solution.py:29
  59.1 1.0 copy-start.3
  60.1 24.4 %collective-permute-start.2 = (bf16[15,128,256]{2,1,0:T(8,128)(2,1)S(1)}, bf16[15,128,256]{2,1,0:T(8,128)(2,1)}, u32[]{:S(2)}, u32[]{:S(2)}) collective-permute-start(bf16[15,128,256]{2,1,0:T(8,128)(2,1)S(1)} %collective-permute-done.1), channel_id=1, source_target_pairs={{0,1},{1,2},{2,3},{3,4},{4,5},{5,6},{6,7},{7,0},{8,9},{9,10},{10,1... | collective-permute-start | bytes 2949128 | tf_op jit(solution)/shard_map/ppermute | solution.py:26
  62.0 25.4 %collective-permute-start.5 = (bf16[15,128,256]{2,1,0:T(8,128)(2,1)}, bf16[15,128,256]{2,1,0:T(8,128)(2,1)}, u32[]{:S(2)}, u32[]{:S(2)}) collective-permute-start(bf16[15,128,256]{2,1,0:T(8,128)(2,1)} %collective-permute-done.4), channel_id=1, source_target_pairs={{1,0},{2,1},{3,2},{4,3},{5,4},{6,5},{7,6},{0,7},{9,8},{10,9},{11,1... | collective-permute-start | bytes 2949128 | tf_op jit(solution)/shard_map/ppermute | solution.py:29
  84.5 23.8 %collective-permute-start.3 = (bf16[15,128,256]{2,1,0:T(8,128)(2,1)}, bf16[15,128,256]{2,1,0:T(8,128)(2,1)}, u32[]{:S(2)}, u32[]{:S(2)}) collective-permute-start(bf16[15,128,256]{2,1,0:T(8,128)(2,1)} %collective-permute-done.2), channel_id=1, source_target_pairs={{0,1},{1,2},{2,3},{3,4},{4,5},{5,6},{6,7},{7,0},{8,9},{9,10},{10,1... | collective-permute-start | bytes 2949128 | tf_op jit(solution)/shard_map/ppermute | solution.py:26
  87.4 34.2 %collective-permute-start.6 = (bf16[15,128,256]{2,1,0:T(8,128)(2,1)}, bf16[15,128,256]{2,1,0:T(8,128)(2,1)S(1)}, u32[]{:S(2)}, u32[]{:S(2)}) collective-permute-start(bf16[15,128,256]{2,1,0:T(8,128)(2,1)} %collective-permute-done.5), channel_id=1, source_target_pairs={{1,0},{2,1},{3,2},{4,3},{5,4},{6,5},{7,6},{0,7},{9,8},{10,9},{11,1... | collective-permute-start | bytes 2949128 | tf_op jit(solution)/shard_map/ppermute | solution.py:29
  130.4 10.7 %copy-start.1 = (bf16[15,128,256]{2,1,0:T(8,128)(2,1)S(1)}, bf16[15,128,256]{2,1,0:T(8,128)(2,1)}, u32[]{:S(2)}) copy-start(bf16[15,128,256]{2,1,0:T(8,128)(2,1)} %param.8) | copy-start | bytes 2949124
  148.0 18.7 %copy-start.4 = (s32[960]{0:T(1024)S(1)}, s32[960]{0:T(1024)}, u32[]{:S(2)}) copy-start(s32[960]{0:T(1024)} %param.14) | copy-start | bytes 11524
  148.0 18.7 %copy-start.5 = (s32[960]{0:T(1024)S(1)}, s32[960]{0:T(1024)}, u32[]{:S(2)}) copy-start(s32[960]{0:T(1024)} %param.13) | copy-start | bytes 11524
  148.0 116.5 %copy-start.7 = (f32[256,8]{0,1:T(8,128)S(1)}, f32[256,8]{0,1:T(8,128)}, u32[]{:S(2)}) copy-start(f32[256,8]{0,1:T(8,128)} %param.12) | copy-start | bytes 24580
  148.0 116.5 %copy-start.8 = (f32[256]{0:T(256)S(1)}, f32[256]{0:T(256)}, u32[]{:S(2)}) copy-start(f32[256]{0:T(256)} %param.11) | copy-start | bytes 3076
  152.4 117.2 %copy-start.6 = (s32[384]{0:T(512)S(1)}, s32[384]{0:T(512)}, u32[]{:S(2)}) copy-start(s32[384]{0:T(512)} %param.15) | copy-start | bytes 4612
  152.4 109.0 %all-to-all-start = ((bf16[64,128,256]{2,1,0:T(8,128)(2,1)}), bf16[64,128,256]{2,1,0:T(8,128)(2,1)}, u32[]{:S(2)}, u32[]{:S(2)}) async-start(bf16[64,128,256]{2,1,0:T(8,128)(2,1)} %copy.41), calls=%async_computation | async-start | bytes 8388608 | tf_op jit(solution)/shard_map/all_to_all | solution.py:117
  266.2 15.2 %all-to-all-start.1 = ((f32[8,1,11520]{2,1,0:T(1,128)}), f32[8,1,11520]{2,1,0:T(1,128)S(1)}, u32[]{:S(2)}, u32[]{:S(2)}) async-start(f32[8,1,11520]{2,1,0:T(1,128)} %broadcast_in_dim.90), calls=%async_computation.1 | async-start | bytes 737280 | tf_op jit(solution)/shard_map/all_to_all | solution.py:44
  283.4 22.6 %all-to-all-start.2 = ((f32[64,6,8]{2,1,0:T(8,128)}), f32[64,6,8]{2,1,0:T(8,128)S(1)}, u32[]{:S(2)}, u32[]{:S(2)}) async-start(f32[64,6,8]{2,1,0:T(8,128)} %copy.44), calls=%async_computation.2 | async-start | bytes 524288 | tf_op jit(solution)/shard_map/all_to_all | solution.py:67
